TPU v7x, 32 devices: a whole 2x2x4 slice. The times are simulated.
32 devices in a mesh: fsdp: 4 (over z), tp: 8 (over y, x, core).
Axes of the slice: x: 2, y: 2, z: 4, core: 2. Of those that a mesh axis runs over, the one named last changes fastest.
Arguments:
- tokens: bfloat16 [3008, 4096], P('fsdp', 'tp'), may hold values from -6 to 6
- norm_gain: float32 [4096], replicated, may hold values from 0.5 to 1.5
- base_gate: bfloat16 [4096, 12288], P(None, 'tp'), may hold values from -0.09375 to 0.09375
- base_up: bfloat16 [4096, 12288], P(None, 'tp'), may hold values from -0.09375 to 0.09375
- base_down: bfloat16 [12288, 4096], P('tp'), may hold values from -0.0546875 to 0.0546875
- code_gate: bfloat16 [4096, 12288], P(('fsdp', 'tp')), may hold values from -4 to 4
- code_up: bfloat16 [4096, 12288], P(('fsdp', 'tp')), may hold values from -4 to 4
- scale_gate: float32 [4096, 96], P(('fsdp', 'tp')), may hold values from 0.005 to 0.05
- scale_up: float32 [4096, 96], P(('fsdp', 'tp')), may hold values from 0.005 to 0.05
- code_down: bfloat16 [12288, 4096], P(None, ('fsdp', 'tp')), may hold values from -4 to 4
- scale_down: float32 [96, 4096], P(None, ('fsdp', 'tp')), may hold values from 0.005 to 0.05
- cu_seqlens: int32 [4, 9], P('fsdp'), may hold values from 0 to 752, as said below
Outputs:
- mixed: bfloat16 [3008, 4096], P('fsdp', 'tp')
- seq_means: float32 [32, 4096], P('fsdp', 'tp')
Inputs may be any that keep to these rules, and one draw needn't show every extreme that they name: `cu_seqlens`: each row starts at 0 and rises strictly; its last entry is the group's live tokens, which fill the first slots of its 752. Over all groups the live tokens add up to exactly 1536, and some group has exactly 752.
All inputs are finite; a program needn't handle non-finite values.
Results may differ from a plain program's by a relative error of at most 0.023.
Values may be sent and summed in bfloat16 or wider, within the bound.
A program may use at most 256 MiB of HBM per device.

v0:
```python
import jax
import jax.numpy as jnp
from jax import lax
from jax.sharding import PartitionSpec as P

SEQS = 8
EPSILON = 1e-06


def dequant_rows(base_part, code_part, scales):
    height, breadth = code_part.shape
    blocks = scales.shape[1]
    spread_out = (
        code_part.astype(jnp.float32).reshape(height, blocks, breadth // blocks)
        * scales[:, :, None]
    )
    return (base_part.astype(jnp.float32) + spread_out.reshape(height, breadth)).astype(
        jnp.bfloat16
    )


def dequant_cols(base_part, code_part, scales):
    height, breadth = code_part.shape
    blocks = scales.shape[0]
    spread_out = (
        code_part.astype(jnp.float32).reshape(blocks, height // blocks, breadth)
        * scales[:, None, :]
    )
    return (base_part.astype(jnp.float32) + spread_out.reshape(height, breadth)).astype(
        jnp.bfloat16
    )


def forward(
    rows_in,
    norm_gain,
    base_gate,
    base_up,
    base_down,
    code_gate,
    code_up,
    scale_gate,
    scale_up,
    code_down,
    scale_down,
):
    gathered = lax.all_gather(rows_in, "tp", axis=1, tiled=True)
    widened = gathered.astype(jnp.float32)
    inverse = lax.rsqrt(jnp.mean(widened * widened, axis=1, keepdims=True) + EPSILON)
    normed = (widened * inverse * norm_gain[None, :]).astype(jnp.bfloat16)
    sliced = (
        lax.all_to_all(code_gate, "tp", split_axis=1, concat_axis=0, tiled=True),
        lax.all_to_all(code_up, "tp", split_axis=1, concat_axis=0, tiled=True),
        lax.all_to_all(
            scale_gate.astype(jnp.bfloat16), "tp", split_axis=1, concat_axis=0, tiled=True
        ).astype(scale_gate.dtype),
        lax.all_to_all(
            scale_up.astype(jnp.bfloat16), "tp", split_axis=1, concat_axis=0, tiled=True
        ).astype(scale_up.dtype),
    )
    pieces = (
        lax.all_gather(sliced[0], "fsdp", axis=0, tiled=True),
        lax.all_gather(sliced[1], "fsdp", axis=0, tiled=True),
        lax.all_gather(sliced[2].astype(jnp.bfloat16), "fsdp", axis=0, tiled=True).astype(
            jnp.float32
        ),
        lax.all_gather(sliced[3].astype(jnp.bfloat16), "fsdp", axis=0, tiled=True).astype(
            jnp.float32
        ),
    )
    gate_add = jnp.dot(
        normed, dequant_rows(base_gate, pieces[0], pieces[2]), preferred_element_type=jnp.float32
    )
    up_add = jnp.dot(
        normed, dequant_rows(base_up, pieces[1], pieces[3]), preferred_element_type=jnp.float32
    )
    hidden = (jax.nn.silu(gate_add) * up_add).astype(jnp.bfloat16)
    sliced_down = (
        lax.all_to_all(code_down, "tp", split_axis=0, concat_axis=1, tiled=True),
        lax.all_to_all(
            scale_down.astype(jnp.bfloat16), "tp", split_axis=0, concat_axis=1, tiled=True
        ).astype(scale_down.dtype),
    )
    pieces = (
        lax.all_gather(sliced_down[0], "fsdp", axis=1, tiled=True),
        lax.all_gather(sliced_down[1].astype(jnp.bfloat16), "fsdp", axis=1, tiled=True).astype(
            jnp.float32
        ),
    )
    block_out = jnp.dot(
        hidden, dequant_cols(base_down, pieces[0], pieces[1]), preferred_element_type=jnp.float32
    )
    summed = lax.psum_scatter(
        block_out.astype(jnp.bfloat16), "tp", scatter_dimension=1, tiled=True
    ).astype(jnp.float32)
    return (rows_in.astype(jnp.float32) + summed).astype(jnp.bfloat16)


def shards(
    tokens,
    norm_gain,
    base_gate,
    base_up,
    base_down,
    code_gate,
    code_up,
    scale_gate,
    scale_up,
    code_down,
    scale_down,
    cu_seqlens,
):
    capacity = tokens.shape[0]
    bounds = cu_seqlens[0]
    live_count = bounds[SEQS]
    positions = jnp.arange(capacity, dtype=jnp.int32)
    mixed_rows = forward(
        tokens,
        norm_gain,
        base_gate,
        base_up,
        base_down,
        code_gate,
        code_up,
        scale_gate,
        scale_up,
        code_down,
        scale_down,
    )
    mixed_rows = jnp.where(
        (positions < live_count)[:, None], mixed_rows, jnp.zeros((), jnp.bfloat16)
    )
    member = (positions[None, :] >= bounds[:-1, None]) & (positions[None, :] < bounds[1:, None])
    seq_sums = jnp.dot(member.astype(jnp.bfloat16), mixed_rows, preferred_element_type=jnp.float32)
    lengths = (bounds[1:] - bounds[:-1]).astype(jnp.float32)
    return (mixed_rows, seq_sums / lengths[:, None])


def solution(mesh):
    placed = (
        P("fsdp", "tp"),
        P(),
        P(None, "tp"),
        P(None, "tp"),
        P("tp", None),
        P(("fsdp", "tp"), None),
        P(("fsdp", "tp"), None),
        P(("fsdp", "tp"), None),
        P(("fsdp", "tp"), None),
        P(None, ("fsdp", "tp")),
        P(None, ("fsdp", "tp")),
        P("fsdp", None),
    )
    return jax.shard_map(
        shards,
        mesh=mesh,
        in_specs=placed,
        out_specs=(P("fsdp", "tp"), P("fsdp", "tp")),
        check_vma=False,
    )
```

profile of v0, /device:TPU:0, one launch (start us, length us, event | category | flops | bytes accessed | tf_op | source)
XLA Modules:
  0.0 834.5 jit_solution(9441921378246151597)
XLA Ops:
  7.9 3.5 copy.26
  11.4 57.3 %all_to_all.114 = bf16[128,8,1536]{0,2,1:T(8,128)(2,1)S(1)} all-to-all(bf16[128,8,1536]{0,2,1:T(8,128)(2,1)S(1)} %bitcast.81), channel_id=1, replica_groups=mesh['fsdp'=4,'tp'=8] {'tp'}, dimensions={1} | all-to-all | bytes 6291456 | tf_op jit(solution)/shard_map/all_to_all | solution.py:52
  71.0 3.5 copy.30
  74.4 40.3 %all_to_all.115 = bf16[128,8,1536]{0,2,1:T(8,128)(2,1)S(1)} all-to-all(bf16[128,8,1536]{0,2,1:T(8,128)(2,1)S(1)} %bitcast.82), channel_id=1, replica_groups=mesh['fsdp'=4,'tp'=8] {'tp'}, dimensions={1} | all-to-all | bytes 6291456 | tf_op jit(solution)/shard_map/all_to_all | solution.py:53
  116.9 41.4 %all_to_all.116 = bf16[8,1536,128]{2,1,0:T(8,128)(2,1)S(1)} all-to-all(bf16[8,1536,128]{2,1,0:T(8,128)(2,1)} %bitcast.83), channel_id=1, replica_groups=mesh['fsdp'=4,'tp'=8] {'tp'}, dimensions={0} | all-to-all | bytes 6291456 | tf_op jit(solution)/shard_map/all_to_all | solution.py:79
  161.1 3.3 all-to-all-start.1
  164.5 16.8 %copy.25 = bf16[4096,1536]{0,1:T(8,128)(2,1)} copy(bf16[4096,1536]{1,0:T(8,128)(2,1)} %param.14) | data formatting | bytes 25165824 | tf_op args[2]
  181.3 16.1 %copy.29 = bf16[4096,1536]{0,1:T(8,128)(2,1)} copy(bf16[4096,1536]{1,0:T(8,128)(2,1)} %param.15) | data formatting | bytes 25165824 | tf_op args[3]
  198.6 4.2 all-to-all-start.3
  202.9 22.0 %all_gather.23 = bf16[4096,12]{0,1:T(8,128)(2,1)S(1)} all-gather(bf16[1024,12]{0,1:T(8,128)(2,1)S(1)} %bitcast.84), channel_id=1, replica_groups=mesh['fsdp'=4,'tp'=8] {'fsdp'}, dimensions={0}, use_global_device_ids=true | all-gather | bytes 122880 | tf_op jit(solution)/shard_map/all_gather | solution.py:64
  224.9 4.0 all-to-all-start.5
  229.0 26.2 %all_gather.25 = bf16[4096,12]{0,1:T(8,128)(2,1)S(1)} all-gather(bf16[1024,12]{0,1:T(8,128)(2,1)S(1)} %bitcast.85), channel_id=1, replica_groups=mesh['fsdp'=4,'tp'=8] {'fsdp'}, dimensions={0}, use_global_device_ids=true | all-gather | bytes 122880 | tf_op jit(solution)/shard_map/all_gather | solution.py:67
  255.3 19.9 %all_gather.27 = bf16[12,4096]{1,0:T(8,128)(2,1)S(1)} all-gather(bf16[12,1024]{1,0:T(8,128)(2,1)S(1)} %bitcast.86), channel_id=1, replica_groups=mesh['fsdp'=4,'tp'=8] {'fsdp'}, dimensions={1}, use_global_device_ids=true | all-gather | bytes 122880 | tf_op jit(solution)/shard_map/all_gather | solution.py:86
  275.3 4.0 fusion.6
  279.3 28.5 %all-gather.7.cloned.1.call-done = bf16[4096,1536]{0,1:T(8,128)(2,1)} async-done(((bf16[1024,1536]{0,1:T(8,128)(2,1)}), bf16[4096,1536]{0,1:T(8,128)(2,1)}) %all-gather.7.cloned.1.call-update) | async-done | bytes 12582928 | tf_op jit(solution)/shard_map/all_gather | solution.py:62
  307.8 16.4 %fusion.5 = bf16[4096,1536]{0,1:T(8,128)(2,1)} fusion(bf16[4096,1536]{0,1:T(8,128)(2,1)} %all-gather.7.cloned.1.call-done, bf16[4096,1536]{0,1:T(8,128)(2,1)} %copy.25, f32[4096,12]{0,1:T(8,128)S(1)} %convert_element_type.86), kind=kLoop, calls=%fused_computation.8 | loop fusion | flops 31457280 | bytes 37945344 | tf_op jit(solution)/shard_map/convert_element_type | solution.py:17
  324.2 201.6 %all-gather.9.cloned.1.call-done = bf16[4096,1536]{0,1:T(8,128)(2,1)} async-done(((bf16[1024,1536]{0,1:T(8,128)(2,1)}), bf16[4096,1536]{0,1:T(8,128)(2,1)}) %all-gather.9.cloned.1.call-update) | async-done | bytes 12582928 | tf_op jit(solution)/shard_map/all_gather | solution.py:63
  525.8 16.8 %fusion.3 = bf16[4096,1536]{0,1:T(8,128)(2,1)} fusion(bf16[4096,1536]{0,1:T(8,128)(2,1)} %all-gather.9.cloned.1.call-done, bf16[4096,1536]{0,1:T(8,128)(2,1)} %copy.29, f32[4096,12]{0,1:T(8,128)S(1)} %convert_element_type.91), kind=kLoop, calls=%fused_computation.5 | loop fusion | flops 31457280 | bytes 37945344 | tf_op jit(solution)/shard_map/convert_element_type | solution.py:17
  544.3 13.5 %fusion.12 = f32[752,1536]{1,0:T(8,128)} fusion(bf16[4096,1536]{0,1:T(8,128)(2,1)S(1)} %copy-done, bf16[752,4096]{1,0:T(8,128)(2,1)} %all-gather.5.cloned.1.call-done, f32[4096]{0:T(1024)S(1)} %copy-done.7, f32[752]{0:T(1024)S(1)} %add_rsqrt_fusion), kind=kOutput, calls=%fused_computation.20 | convolution fusion | flops 9474670592 | bytes 23382976 | tf_op jit(solution)/shard_map/dot_general | solution.py:71
  557.8 16.7 %multiply_convert_fusion.clone.4 = bf16[752,1536]{1,0:T(8,128)(2,1)} fusion(f32[752,1536]{1,0:T(8,128)} %fusion.12, bf16[4096,1536]{0,1:T(8,128)(2,1)} %fusion.3, bf16[752,4096]{1,0:T(8,128)(2,1)} %all-gather.5.cloned.1.call-done, f32[4096]{0:T(1024)S(1)} %copy-done.7, f32[752]{0:T(1024)S(1)} %add_rsqrt_fusion), kind=kOutput, calls=%fused_computation.15.clone.clone.clone.1 | convolution fusion | flops 9481601024 | bytes 25693120 | tf_op jit(solution)/shard_map/dot_general | solution.py:74
  574.5 169.1 %all-gather.11.cloned.1.call-done = bf16[1536,4096]{1,0:T(8,128)(2,1)} async-done(((bf16[1536,1024]{1,0:T(8,128)(2,1)}), bf16[1536,4096]{1,0:T(8,128)(2,1)}) %all-gather.11.cloned.1.call-update) | async-done | bytes 12582928 | tf_op jit(solution)/shard_map/all_gather | solution.py:85
  743.6 11.4 %fusion.1 = bf16[1536,4096]{1,0:T(8,128)(2,1)S(1)} fusion(bf16[1536,4096]{1,0:T(8,128)(2,1)} %all-gather.11.cloned.1.call-done, bf16[1536,4096]{1,0:T(8,128)(2,1)} %param.16, f32[12,4096]{1,0:T(8,128)S(1)} %convert_element_type.97), kind=kLoop, calls=%fused_computation.2 | loop fusion | flops 31457280 | bytes 37945344 | tf_op jit(solution)/shard_map/convert_element_type | solution.py:29
  755.1 11.5 %convolution_convert_fusion = bf16[752,4096]{1,0:T(8,128)(2,1)} fusion(bf16[1536,4096]{1,0:T(8,128)(2,1)S(1)} %fusion.1, bf16[752,1536]{1,0:T(8,128)(2,1)S(1)} %copy-done.8), kind=kOutput, calls=%fused_computation.14 | convolution fusion | flops 9465430016 | bytes 21053440 | tf_op jit(solution)/shard_map/dot_general | solution.py:90
  768.0 57.7 %reduce-scatter.2.cloned.1.call-done = bf16[752,512]{1,0:T(8,128)(2,1)} async-done(((bf16[752,4096]{1,0:T(8,128)(2,1)}), bf16[752,512]{1,0:T(8,128)(2,1)}) %reduce-scatter.2.cloned.1.call-update) | async-done | bytes 770064 | tf_op jit(solution)/shard_map/reduce_scatter | solution.py:93
  (60 shorter events, 14.8 us)
Async XLA Ops:
  7.2 268.1 %all-gather.5.cloned.1.call-start = ((), (), s32[]{:S(2)}) async-start(), calls=%async_computation.7 | async-start | bytes 6930432 | tf_op jit(solution)/shard_map/all_gather | solution.py:47
  7.9 299.9 %all-gather.7.cloned.1.call-start = ((), (), s32[]{:S(2)}) async-start(), calls=%async_computation.8 | async-start | bytes 15728640 | tf_op jit(solution)/shard_map/all_gather | solution.py:62
  70.9 454.9 %all-gather.9.cloned.1.call-start = ((), (), s32[]{:S(2)}) async-start(), calls=%async_computation.9 | async-start | bytes 15728640 | tf_op jit(solution)/shard_map/all_gather | solution.py:63
  114.7 45.8 %copy-start.3 = (f32[128,96]{0,1:T(8,128)S(1)}, f32[128,96]{0,1:T(8,128)}, u32[]{:S(2)}) copy-start(f32[128,96]{0,1:T(8,128)} %param.19) | copy-start | bytes 147460
  116.9 626.8 %all-gather.11.cloned.1.call-start = ((), (), s32[]{:S(2)}) async-start(), calls=%async_computation.10 | async-start | bytes 15728640 | tf_op jit(solution)/shard_map/all_gather | solution.py:85
  161.1 37.5 %all-to-all-start.1 = ((bf16[128,8,12]{0,2,1:T(8,128)(2,1)}), bf16[128,8,12]{0,2,1:T(8,128)(2,1)S(1)}, u32[]{:S(2)}, u32[]{:S(2)}) async-start(bf16[128,8,12]{0,2,1:T(8,128)(2,1)} %all_to_all.88), calls=%async_computation.1 | async-start | bytes 65536 | tf_op jit(solution)/shard_map/all_to_all | solution.py:54
  181.3 16.1 %copy-start.4 = (f32[128,96]{0,1:T(8,128)S(1)}, f32[128,96]{0,1:T(8,128)}, u32[]{:S(2)}) copy-start(f32[128,96]{0,1:T(8,128)} %param.20) | copy-start | bytes 147460
  181.3 16.7 %copy-start.5 = (f32[96,128]{1,0:T(8,128)S(1)}, f32[96,128]{1,0:T(8,128)}, u32[]{:S(2)}) copy-start(f32[96,128]{1,0:T(8,128)} %param.22) | copy-start | bytes 147460
  198.6 26.2 %all-to-all-start.3 = ((bf16[128,8,12]{0,2,1:T(8,128)(2,1)}), bf16[128,8,12]{0,2,1:T(8,128)(2,1)S(1)}, u32[]{:S(2)}, u32[]{:S(2)}) async-start(bf16[128,8,12]{0,2,1:T(8,128)(2,1)} %all_to_all.96), calls=%async_computation.3 | async-start | bytes 65536 | tf_op jit(solution)/shard_map/all_to_all | solution.py:57
  224.9 30.4 %all-to-all-start.5 = ((bf16[8,12,128]{2,1,0:T(8,128)(2,1)}), bf16[8,12,128]{2,1,0:T(8,128)(2,1)S(1)}, u32[]{:S(2)}, u32[]{:S(2)}) async-start(bf16[8,12,128]{2,1,0:T(8,128)(2,1)} %all_to_all.104), calls=%async_computation.5 | async-start | bytes 65536 | tf_op jit(solution)/shard_map/all_to_all | solution.py:80
  228.9 596.8 %reduce-scatter.2.cloned.1.call-start = ((), (), s32[]{:S(2)}) async-start(), calls=%async_computation.11 | async-start | bytes 6930432 | tf_op jit(solution)/shard_map/reduce_scatter | solution.py:93
  324.2 218.4 %copy-start.7 = (f32[4096]{0:T(1024)S(1)}, f32[4096]{0:T(1024)}, u32[]{:S(2)}) copy-start(f32[4096]{0:T(1024)} %param.13) | copy-start | bytes 49156
  525.8 18.5 %copy-start = (bf16[4096,1536]{0,1:T(8,128)(2,1)S(1)}, bf16[4096,1536]{0,1:T(8,128)(2,1)}, u32[]{:S(2)}) copy-start(bf16[4096,1536]{0,1:T(8,128)(2,1)} %fusion.5) | copy-start | bytes 37748740
  743.6 11.4 %copy-start.8 = (bf16[752,1536]{1,0:T(8,128)(2,1)S(1)}, bf16[752,1536]{1,0:T(8,128)(2,1)}, u32[]{:S(2)}) copy-start(bf16[752,1536]{1,0:T(8,128)(2,1)} %multiply_convert_fusion.clone.4) | copy-start | bytes 6930436
  755.0 11.6 %copy-start.6 = (s32[1,9]{1,0:T(1,128)S(1)}, s32[1,9]{1,0:T(1,128)}, u32[]{:S(2)}) copy-start(s32[1,9]{1,0:T(1,128)} %param.23) | copy-start | bytes 112
  755.1 70.7 %copy-start.1 = (bf16[752,512]{1,0:T(8,128)(2,1)S(1)}, bf16[752,512]{1,0:T(8,128)(2,1)}, u32[]{:S(2)}) copy-start(bf16[752,512]{1,0:T(8,128)(2,1)} %param.12) | copy-start | bytes 2310148
  827.1 0.9 copy-start.2
Sparse Core Ops, SparseCore 0:
  9.8 71.2 all-gather.4
  82.7 225.0 all-gather.6
  309.4 216.4 all-gather.8
  527.2 216.3 all-gather.10
  766.7 58.9 reduce-scatter.1
where the time goes:
time: 836 us; the launch traced here: 835 us
  waiting for transfers between devices  458 us (55%)
  blocking collectives  207 us (25%)
  other arithmetic  50.8 us (6%)
  local copies, waits for them, and re-layouts  50.6 us (6%)
  matrix products  42.6 us (5%)
  between operations  14 us (2%)
  starting transfers between devices  11.7 us (1%)
    all_gather x1, waiting for transfers between devices, forward(): lax.all_gather(sliced[1], 'fsdp', axis=0, tiled=True)  202 us
    all_gather x1, waiting for transfers between devices, forward(): lax.all_gather(sliced_down[0], 'fsdp', axis=1, tiled=True)  169 us
    reduce_scatter x1, waiting for transfers between devices, forward(): lax.psum_scatter(block_out.astype(jnp.bfloat16), 'tp', scatter_dimension=...  57.7 us
    all_to_all x1, blocking collectives, forward(): lax.all_to_all(code_gate, 'tp', split_axis=1, concat_axis=0, tiled=True)  57.3 us
    unnamed x28, local copies, waits for them, and re-layouts  41.6 us
    all_to_all x1, blocking collectives, forward(): lax.all_to_all(code_down, 'tp', split_axis=0, concat_axis=1, tiled=True)  41.4 us
    all_to_all x1, blocking collectives, forward(): lax.all_to_all(code_up, 'tp', split_axis=1, concat_axis=0, tiled=True)  40.3 us
    convert_element_type x2, other arithmetic, dequant_rows(): (base_part.astype(jnp.float32) + spread_out.reshape(height, breadth)).ast...  33.3 us
  transfers between devices with their start and end apart: 8, of which 4 were waited for; matrix products, arithmetic and copies ran while one was open for 14% of the time, Pallas kernels for 0%

commit v1 on v0

--- a/solution.py
+++ b/solution.py
@@ -5,6 +5,12 @@
 
 SEQS = 8
 EPSILON = 1e-06
+
+
+def stacked_exchange(shard, axis, split, join):
+    parts = jnp.split(shard, lax.axis_size(axis), axis=split)
+    received = lax.all_to_all(jnp.stack(parts), axis, 0, 0)
+    return jnp.concatenate(received, axis=join)
 
 
 def dequant_rows(base_part, code_part, scales):
@@ -49,7 +55,7 @@
     inverse = lax.rsqrt(jnp.mean(widened * widened, axis=1, keepdims=True) + EPSILON)
     normed = (widened * inverse * norm_gain[None, :]).astype(jnp.bfloat16)
     sliced = (
-        lax.all_to_all(code_gate, "tp", split_axis=1, concat_axis=0, tiled=True),
+        stacked_exchange(code_gate, "tp", 1, 0),
         lax.all_to_all(code_up, "tp", split_axis=1, concat_axis=0, tiled=True),
         lax.all_to_all(
             scale_gate.astype(jnp.bfloat16), "tp", split_axis=1, concat_axis=0, tiled=True

time: 836 us -> 839 us (level)
    unnamed x28 -> x36, local copies, waits for them, and re-layouts: 41.6 us -> 46.6 us
where the time goes in v1:
time: 839 us; the launch traced here: 837 us
  waiting for transfers between devices  456 us (54%)
  blocking collectives  205 us (24%)
  local copies, waits for them, and re-layouts  57.4 us (7%)
  other arithmetic  51 us (6%)
  matrix products  42.6 us (5%)
  between operations  14 us (2%)
  starting transfers between devices  11.5 us (1%)
    all_gather x1, waiting for transfers between devices, forward(): lax.all_gather(sliced[1], 'fsdp', axis=0, tiled=True)  201 us
    all_gather x1, waiting for transfers between devices, forward(): lax.all_gather(sliced_down[0], 'fsdp', axis=1, tiled=True)  169 us
    all_to_all x1, blocking collectives, stacked_exchange(): received = lax.all_to_all(jnp.stack(parts), axis, 0, 0)  60.6 us
    reduce_scatter x1, waiting for transfers between devices, forward(): lax.psum_scatter(block_out.astype(jnp.bfloat16), 'tp', scatter_dimension=...  57.1 us
    unnamed x36, local copies, waits for them, and re-layouts  46.6 us
    all_to_all x1, blocking collectives, forward(): lax.all_to_all(code_up, 'tp', split_axis=1, concat_axis=0, tiled=True)  40.3 us
    all_to_all x1, blocking collectives, forward(): lax.all_to_all(code_down, 'tp', split_axis=0, concat_axis=1, tiled=True)  40.3 us
    convert_element_type x2, other arithmetic, dequant_rows(): (base_part.astype(jnp.float32) + spread_out.reshape(height, breadth)).ast...  33.4 us
  transfers between devices with their start and end apart: 8, of which 4 were waited for; matrix products, arithmetic and copies ran while one was open for 14% of the time, Pallas kernels for 0%

profile of v1, /device:TPU:0, one launch (start us, length us, event | category | flops | bytes accessed | tf_op | source)
XLA Modules:
  0.0 837.4 jit_solution(13361525801028013734)
XLA Ops:
  16.2 60.6 %all_to_all.100 = bf16[8,128,1536]{2,1,0:T(8,128)(2,1)S(1)} all-to-all(bf16[8,128,1536]{2,1,0:T(8,128)(2,1)S(1)} %bitcast_dynamic-update-slice_fusion), channel_id=1, replica_groups=mesh['fsdp'=4,'tp'=8] {'tp'}, dimensions={0} | all-to-all | bytes 6291456 | tf_op jit(solution)/shard_map/all_to_all | solution.py:12
  76.7 3.0 copy.33
  79.8 3.5 copy.28
  83.3 40.3 %all_to_all.101 = bf16[128,8,1536]{0,2,1:T(8,128)(2,1)S(1)} all-to-all(bf16[128,8,1536]{0,2,1:T(8,128)(2,1)S(1)} %bitcast.92), channel_id=1, replica_groups=mesh['fsdp'=4,'tp'=8] {'tp'}, dimensions={1} | all-to-all | bytes 6291456 | tf_op jit(solution)/shard_map/all_to_all | solution.py:59
  126.6 40.3 %all_to_all.102 = bf16[8,1536,128]{2,1,0:T(8,128)(2,1)S(1)} all-to-all(bf16[8,1536,128]{2,1,0:T(8,128)(2,1)S(1)} %bitcast.93), channel_id=1, replica_groups=mesh['fsdp'=4,'tp'=8] {'tp'}, dimensions={0} | all-to-all | bytes 6291456 | tf_op jit(solution)/shard_map/all_to_all | solution.py:85
  169.6 3.3 all-to-all-start.1
  173.0 15.9 %copy.24 = bf16[4096,1536]{0,1:T(8,128)(2,1)} copy(bf16[4096,1536]{1,0:T(8,128)(2,1)} %param.14) | data formatting | bytes 25165824 | tf_op args[2]
  188.9 16.9 %copy.27 = bf16[4096,1536]{0,1:T(8,128)(2,1)} copy(bf16[4096,1536]{1,0:T(8,128)(2,1)} %param.15) | data formatting | bytes 25165824 | tf_op args[3]
  207.1 4.1 all-to-all-start.3
  211.2 16.9 %all_gather.23 = bf16[4096,12]{0,1:T(8,128)(2,1)S(1)} all-gather(bf16[1024,12]{0,1:T(8,128)(2,1)S(1)} %bitcast.94), channel_id=1, replica_groups=mesh['fsdp'=4,'tp'=8] {'fsdp'}, dimensions={0}, use_global_device_ids=true | all-gather | bytes 122880 | tf_op jit(solution)/shard_map/all_gather | solution.py:70
  228.2 3.9 all-to-all-start.5
  232.1 27.4 %all_gather.25 = bf16[4096,12]{0,1:T(8,128)(2,1)S(1)} all-gather(bf16[1024,12]{0,1:T(8,128)(2,1)S(1)} %bitcast.95), channel_id=1, replica_groups=mesh['fsdp'=4,'tp'=8] {'fsdp'}, dimensions={0}, use_global_device_ids=true | all-gather | bytes 122880 | tf_op jit(solution)/shard_map/all_gather | solution.py:73
  259.6 19.4 %all_gather.27 = bf16[12,4096]{1,0:T(8,128)(2,1)S(1)} all-gather(bf16[12,1024]{1,0:T(8,128)(2,1)S(1)} %bitcast.96), channel_id=1, replica_groups=mesh['fsdp'=4,'tp'=8] {'fsdp'}, dimensions={1}, use_global_device_ids=true | all-gather | bytes 122880 | tf_op jit(solution)/shard_map/all_gather | solution.py:92
  279.1 4.0 fusion.6
  283.2 27.6 %all-gather.7.cloned.1.call-done = bf16[4096,1536]{0,1:T(8,128)(2,1)} async-done(((bf16[1024,1536]{0,1:T(8,128)(2,1)}), bf16[4096,1536]{0,1:T(8,128)(2,1)}) %all-gather.7.cloned.1.call-update) | async-done | bytes 12582928 | tf_op jit(solution)/shard_map/all_gather | solution.py:68
  310.8 16.5 %fusion.5 = bf16[4096,1536]{0,1:T(8,128)(2,1)} fusion(bf16[4096,1536]{0,1:T(8,128)(2,1)} %all-gather.7.cloned.1.call-done, bf16[4096,1536]{0,1:T(8,128)(2,1)} %copy.24, f32[4096,12]{0,1:T(8,128)S(1)} %convert_element_type.86), kind=kLoop, calls=%fused_computation.8 | loop fusion | flops 31457280 | bytes 37945344 | tf_op jit(solution)/shard_map/convert_element_type | solution.py:23
  327.3 201.5 %all-gather.9.cloned.1.call-done = bf16[4096,1536]{0,1:T(8,128)(2,1)} async-done(((bf16[1024,1536]{0,1:T(8,128)(2,1)}), bf16[4096,1536]{0,1:T(8,128)(2,1)}) %all-gather.9.cloned.1.call-update) | async-done | bytes 12582928 | tf_op jit(solution)/shard_map/all_gather | solution.py:69
  528.8 16.9 %fusion.3 = bf16[4096,1536]{0,1:T(8,128)(2,1)} fusion(bf16[4096,1536]{0,1:T(8,128)(2,1)} %all-gather.9.cloned.1.call-done, bf16[4096,1536]{0,1:T(8,128)(2,1)} %copy.27, f32[4096,12]{0,1:T(8,128)S(1)} %convert_element_type.91), kind=kLoop, calls=%fused_computation.5 | loop fusion | flops 31457280 | bytes 37945344 | tf_op jit(solution)/shard_map/convert_element_type | solution.py:23
  547.3 13.5 %fusion.12 = f32[752,1536]{1,0:T(8,128)} fusion(bf16[4096,1536]{0,1:T(8,128)(2,1)S(1)} %copy-done, bf16[752,4096]{1,0:T(8,128)(2,1)} %all-gather.5.cloned.1.call-done, f32[4096]{0:T(1024)S(1)} %copy-done.8, f32[752]{0:T(1024)S(1)} %add_rsqrt_fusion), kind=kOutput, calls=%fused_computation.19 | convolution fusion | flops 9474670592 | bytes 23382976 | tf_op jit(solution)/shard_map/dot_general | solution.py:77
  560.8 16.7 %multiply_convert_fusion.clone.4 = bf16[752,1536]{1,0:T(8,128)(2,1)} fusion(f32[752,1536]{1,0:T(8,128)} %fusion.12, bf16[4096,1536]{0,1:T(8,128)(2,1)} %fusion.3, bf16[752,4096]{1,0:T(8,128)(2,1)} %all-gather.5.cloned.1.call-done, f32[4096]{0:T(1024)S(1)} %copy-done.8, f32[752]{0:T(1024)S(1)} %add_rsqrt_fusion), kind=kOutput, calls=%fused_computation.15.clone.clone.clone.1 | convolution fusion | flops 9481601024 | bytes 25693120 | tf_op jit(solution)/shard_map/dot_general | solution.py:80
  577.6 169.1 %all-gather.11.cloned.1.call-done = bf16[1536,4096]{1,0:T(8,128)(2,1)} async-done(((bf16[1536,1024]{1,0:T(8,128)(2,1)}), bf16[1536,4096]{1,0:T(8,128)(2,1)}) %all-gather.11.cloned.1.call-update) | async-done | bytes 12582928 | tf_op jit(solution)/shard_map/all_gather | solution.py:91
  746.6 11.4 %fusion.1 = bf16[1536,4096]{1,0:T(8,128)(2,1)S(1)} fusion(bf16[1536,4096]{1,0:T(8,128)(2,1)} %all-gather.11.cloned.1.call-done, bf16[1536,4096]{1,0:T(8,128)(2,1)} %param.16, f32[12,4096]{1,0:T(8,128)S(1)} %convert_element_type.97), kind=kLoop, calls=%fused_computation.2 | loop fusion | flops 31457280 | bytes 37945344 | tf_op jit(solution)/shard_map/convert_element_type | solution.py:35
  758.0 11.4 %convolution_convert_fusion = bf16[752,4096]{1,0:T(8,128)(2,1)} fusion(bf16[1536,4096]{1,0:T(8,128)(2,1)S(1)} %fusion.1, bf16[752,1536]{1,0:T(8,128)(2,1)S(1)} %copy-done.9), kind=kOutput, calls=%fused_computation.14 | convolution fusion | flops 9465430016 | bytes 21053440 | tf_op jit(solution)/shard_map/dot_general | solution.py:96
  771.5 57.1 %reduce-scatter.2.cloned.1.call-done = bf16[752,512]{1,0:T(8,128)(2,1)} async-done(((bf16[752,4096]{1,0:T(8,128)(2,1)}), bf16[752,512]{1,0:T(8,128)(2,1)}) %reduce-scatter.2.cloned.1.call-update) | async-done | bytes 770064 | tf_op jit(solution)/shard_map/reduce_scatter | solution.py:99
  (69 shorter events, 22.2 us)
Async XLA Ops:
  7.2 272.0 %all-gather.5.cloned.1.call-start = ((), (), s32[]{:S(2)}) async-start(), calls=%async_computation.7 | async-start | bytes 6930432 | tf_op jit(solution)/shard_map/all_gather | solution.py:53
  7.9 302.9 %all-gather.7.cloned.1.call-start = ((), (), s32[]{:S(2)}) async-start(), calls=%async_computation.8 | async-start | bytes 15728640 | tf_op jit(solution)/shard_map/all_gather | solution.py:68
  79.7 449.1 %all-gather.9.cloned.1.call-start = ((), (), s32[]{:S(2)}) async-start(), calls=%async_computation.9 | async-start | bytes 15728640 | tf_op jit(solution)/shard_map/all_gather | solution.py:69
  123.5 3.0 copy-start.1
  125.7 620.9 %all-gather.11.cloned.1.call-start = ((), (), s32[]{:S(2)}) async-start(), calls=%async_computation.10 | async-start | bytes 15728640 | tf_op jit(solution)/shard_map/all_gather | solution.py:91
  166.8 2.2 copy-start.4
  169.6 37.4 %all-to-all-start.1 = ((bf16[128,8,12]{0,2,1:T(8,128)(2,1)}), bf16[128,8,12]{0,2,1:T(8,128)(2,1)S(1)}, u32[]{:S(2)}, u32[]{:S(2)}) async-start(bf16[128,8,12]{0,2,1:T(8,128)(2,1)} %all_to_all.74), calls=%async_computation.1 | async-start | bytes 65536 | tf_op jit(solution)/shard_map/all_to_all | solution.py:60
  188.9 16.9 %copy-start.5 = (f32[128,96]{0,1:T(8,128)S(1)}, f32[128,96]{0,1:T(8,128)}, u32[]{:S(2)}) copy-start(f32[128,96]{0,1:T(8,128)} %param.20) | copy-start | bytes 147460
  188.9 17.5 %copy-start.6 = (f32[96,128]{1,0:T(8,128)S(1)}, f32[96,128]{1,0:T(8,128)}, u32[]{:S(2)}) copy-start(f32[96,128]{1,0:T(8,128)} %param.22) | copy-start | bytes 147460
  207.1 21.1 %all-to-all-start.3 = ((bf16[128,8,12]{0,2,1:T(8,128)(2,1)}), bf16[128,8,12]{0,2,1:T(8,128)(2,1)S(1)}, u32[]{:S(2)}, u32[]{:S(2)}) async-start(bf16[128,8,12]{0,2,1:T(8,128)(2,1)} %all_to_all.82), calls=%async_computation.3 | async-start | bytes 65536 | tf_op jit(solution)/shard_map/all_to_all | solution.py:63
  228.2 31.4 %all-to-all-start.5 = ((bf16[8,12,128]{2,1,0:T(8,128)(2,1)}), bf16[8,12,128]{2,1,0:T(8,128)(2,1)S(1)}, u32[]{:S(2)}, u32[]{:S(2)}) async-start(bf16[8,12,128]{2,1,0:T(8,128)(2,1)} %all_to_all.90), calls=%async_computation.5 | async-start | bytes 65536 | tf_op jit(solution)/shard_map/all_to_all | solution.py:86
  232.0 596.5 %reduce-scatter.2.cloned.1.call-start = ((), (), s32[]{:S(2)}) async-start(), calls=%async_computation.11 | async-start | bytes 6930432 | tf_op jit(solution)/shard_map/reduce_scatter | solution.py:99
  327.3 218.4 %copy-start.8 = (f32[4096]{0:T(1024)S(1)}, f32[4096]{0:T(1024)}, u32[]{:S(2)}) copy-start(f32[4096]{0:T(1024)} %param.13) | copy-start | bytes 49156
  528.8 18.5 %copy-start = (bf16[4096,1536]{0,1:T(8,128)(2,1)S(1)}, bf16[4096,1536]{0,1:T(8,128)(2,1)}, u32[]{:S(2)}) copy-start(bf16[4096,1536]{0,1:T(8,128)(2,1)} %fusion.5) | copy-start | bytes 37748740
  746.6 11.4 %copy-start.9 = (bf16[752,1536]{1,0:T(8,128)(2,1)S(1)}, bf16[752,1536]{1,0:T(8,128)(2,1)}, u32[]{:S(2)}) copy-start(bf16[752,1536]{1,0:T(8,128)(2,1)} %multiply_convert_fusion.clone.4) | copy-start | bytes 6930436
  769.4 0.7 copy-start.7
  769.4 59.1 %copy-start.2 = (bf16[752,512]{1,0:T(8,128)(2,1)S(1)}, bf16[752,512]{1,0:T(8,128)(2,1)}, u32[]{:S(2)}) copy-start(bf16[752,512]{1,0:T(8,128)(2,1)} %param.12) | copy-start | bytes 2310148
  830.0 0.9 copy-start.3
Sparse Core Ops, SparseCore 0:
  9.8 74.9 all-gather.4
  86.4 224.3 all-gather.6
  312.3 216.4 all-gather.8
  530.2 216.3 all-gather.10
  769.6 58.9 reduce-scatter.1
